TPU v7x, 128 devices: a whole 4x4x4 slice. The times are simulated.
128 devices in a mesh: row: 8 (over y, core), col: 16 (over z, x).
Axes of the slice: x: 4, y: 4, z: 4, core: 2. Of those that a mesh axis runs over, the one named last changes fastest.
Arguments:
- activations: bfloat16 [8192, 7168], P('col', 'row'), may hold values from -6 to 6
- running_factor: float32 [7168, 7168], P('row', 'col'), as said below
- deltas: bfloat16 [64, 7168, 256], P('col', 'row'), may hold values from -1.5 to 1.5
- samples: int32 [64], P('col'), may hold values from 1 to 64
Outputs:
- updated_factor: float32 [7168, 7168], P('row', 'col')
- panel_factor: float32 [7168, 1024], P('row', 'col')
- solved_slab: float32 [7168, 256], P('row', 'col')
Inputs may be any that keep to these rules, and one draw needn't show every extreme that they name: running_factor is symmetric and its smallest eigenvalue is 0.5 or more.
All inputs are finite; a program needn't handle non-finite values.
Results may differ from a plain program's by a relative error of at most 0.0003.
Values may be sent and summed in bfloat16 or wider, within the bound.
No kernel may reach another device: no remote copies, remote signals or barrier semaphores. Data moves between devices by JAX's collectives and lax.ppermute only.
A program may use at most 128 MiB of HBM per device.

v0:
```python
import jax
import jax.numpy as jnp
from jax import lax
from jax.sharding import Mesh
from jax.sharding import PartitionSpec as P

TILE = 64
PANEL = 512
PANELS = 2
SHOTS = 64
COL = ("col_0", "col_1")
DECAY = 0.75
DAMPING = 0.05


def joined_along(parts, dim):
    parts = jnp.moveaxis(parts, 0, dim)
    lengths = parts.shape
    return parts.reshape(*lengths[:dim], lengths[dim] * lengths[dim + 1], *lengths[dim + 2 :])


def copy_for_each(shard, axis):
    size = lax.axis_size(axis)
    return lax.all_to_all(
        jnp.broadcast_to(shard[None], (size, *shard.shape)), axis, 0, 0, tiled=True
    )


def gather_directly(shard, axis, dim):
    return joined_along(copy_for_each(shard, axis), dim)


def from_root(shard, axis, root):
    return lax.dynamic_index_in_dim(lax.all_gather(shard, axis), root, 0, keepdims=False)


def filled_up(lines, size):
    spare = -len(lines) % size
    return jnp.pad(lines, [(0, spare)] + [(0, 0)] * (lines.ndim - 1))


def spread_2(shard, axis, root):
    lines = jnp.where(lax.axis_index(axis) == root, shard, jnp.zeros_like(shard)).reshape(
        -1, *shard.shape[1:][-1:]
    )
    padded = filled_up(lines, lax.axis_size(axis))
    own = lax.psum_scatter(padded, axis, scatter_dimension=0, tiled=True)
    return lax.all_gather(own, axis, axis=0, tiled=True)[: len(lines)].reshape(shard.shape)


def gather_axes(shard, axes, dim):
    whole = shard
    for number in range(len(axes) - 1, -1, -1):
        whole = lax.all_gather(whole, axes[number], axis=dim, tiled=True)
    return whole


def canon_rows(stored, group_size):
    trailing_shape = stored.shape[1:]
    blocks = stored.reshape((group_size, -1, TILE) + trailing_shape)
    return jnp.swapaxes(blocks, 0, 1).reshape((-1,) + trailing_shape)


def own_rows(canon, group_size, row_index):
    trailing_shape = canon.shape[1:]
    blocks = canon.reshape((-1, group_size, TILE) + trailing_shape)
    picked = lax.dynamic_index_in_dim(blocks, row_index, 1, keepdims=False)
    return picked.reshape((-1,) + trailing_shape)


def dot_high(left, right):
    return jnp.dot(left, right, precision=lax.Precision.HIGHEST)


def dot_transposed(left, right):
    return lax.dot_general(left, right, (((1,), (1,)), ((), ())), precision=lax.Precision.HIGHEST)


def diagonal_rows(panel_cols, panel_num, row_count):
    per_device = PANEL // TILE // row_count
    first_tile = panel_num * per_device
    local_rows = panel_cols[first_tile * TILE : (first_tile + per_device) * TILE]
    gathered = gather_directly(local_rows, "row", 0)
    return canon_rows(gathered, row_count)


def factor_rows(panel_cols, diag_block, first_row, row_global):
    lower_part = jnp.linalg.cholesky(diag_block)
    below = lax.linalg.triangular_solve(
        lower_part, panel_cols, left_side=False, lower=True, transpose_a=True
    )
    return (jnp.where((row_global >= first_row)[:, None], below, 0.0), lower_part)


def trailing_update(factor, stripe_cols, col_index, row_count, col_count):
    rounds = stripe_cols.reshape(-1, col_count // row_count, TILE, stripe_cols.shape[1])
    picked = lax.dynamic_index_in_dim(rounds, col_index // row_count, 1, keepdims=False)
    picked = picked.reshape(-1, stripe_cols.shape[1])
    column_rows = from_root(picked, "row", col_index % row_count)
    return factor - dot_transposed(stripe_cols, column_rows)


def on_device(activations, running_factor, deltas, samples):
    row_count = lax.axis_size("row")
    col_count = lax.axis_size(COL)
    row_index = lax.axis_index("row")
    col_index = lax.axis_index(COL)
    stripe = running_factor.shape[0]
    local_cols = running_factor.shape[1]
    spread = col_count // row_count
    row_local = jnp.arange(stripe, dtype=jnp.int32)
    col_local = jnp.arange(local_cols, dtype=jnp.int32)
    row_global = (row_local // TILE * row_count + row_index) * TILE + row_local % TILE
    col_global = (col_local // TILE * col_count + col_index) * TILE + col_local % TILE
    all_tokens = lax.all_gather(activations, COL, axis=0, tiled=True)
    tokens = all_tokens.shape[0]
    rounds = all_tokens.reshape(tokens, -1, spread, TILE)
    picked = lax.dynamic_index_in_dim(rounds, col_index // row_count, 2, keepdims=False).reshape(
        tokens, local_cols
    )
    column_feats = spread_2(picked, "row", col_index % row_count)
    gram_tile = lax.dot_general(
        all_tokens, column_feats, (((0,), (0,)), ((), ())), preferred_element_type=jnp.float32
    )
    identity = (row_global[:, None] == col_global[None, :]).astype(jnp.float32)
    factor = DECAY * running_factor + (1.0 - DECAY) / tokens * gram_tile + DAMPING * identity
    stripes = []
    lowers = []
    lead_width = PANELS * PANEL // col_count
    gathered = gather_axes(factor[:, :lead_width], COL, 1)
    early = jnp.swapaxes(gathered.reshape(stripe, col_count, -1, TILE), 1, 2).reshape(
        stripe, PANELS * PANEL
    )
    panel_zero = early[:, :PANEL]
    block_zero = diagonal_rows(panel_zero, 0, row_count)
    stripe_zero, lower_zero = factor_rows(panel_zero, block_zero, 0, row_global)
    per_rows = PANEL // row_count
    prior_rows, block_rows = (
        lax.all_gather(stripe_zero[per_rows : 2 * per_rows], "row", axis=0, tiled=True),
        lax.all_gather(
            early[per_rows : 2 * per_rows, PANEL : 2 * PANEL], "row", axis=0, tiled=True
        ),
    )
    prior = canon_rows(prior_rows, row_count)
    block_one = canon_rows(block_rows, row_count) - dot_transposed(prior, prior)
    panel_one = early[:, PANEL : 2 * PANEL] - dot_transposed(stripe_zero, prior)
    stripe_one, lower_one = factor_rows(panel_one, block_one, PANEL, row_global)
    factor = trailing_update(factor, stripe_zero, col_index, row_count, col_count)
    factor = trailing_update(factor, stripe_one, col_index, row_count, col_count)
    stripes = [stripe_zero, stripe_one]
    lowers = [lower_zero, lower_one]
    both_cols = jnp.concatenate(stripes, 1)
    width_out = both_cols.shape[1] // col_count
    panel_out = lax.dynamic_slice_in_dim(both_cols, col_index * width_out, width_out, 1)
    weights = (samples.astype(jnp.float32) / SHOTS).astype(jnp.bfloat16)
    partial_value = jnp.einsum("k,kmn->mn", weights, deltas, preferred_element_type=jnp.float32)
    slab_cols = lax.psum_scatter(partial_value, COL, scatter_dimension=1, tiled=True)
    done_rows = PANELS * PANEL // row_count
    per_rows = PANEL // row_count
    remainder = slab_cols
    pieces = []
    for panel_num in range(PANELS):
        rows_here = remainder[panel_num * per_rows : (panel_num + 1) * per_rows]
        gathered_rhs = lax.all_gather(rows_here, "row", axis=0, tiled=True)
        solved_part = lax.linalg.triangular_solve(
            lowers[panel_num], canon_rows(gathered_rhs, row_count), left_side=True, lower=True
        )
        remainder = remainder - dot_high(stripes[panel_num], solved_part)
        pieces.append(own_rows(solved_part, row_count, row_index))
    solved = jnp.concatenate(pieces + [remainder[done_rows:]], 0)
    return (factor, panel_out, solved)


def solution(mesh):
    finer = Mesh(mesh.devices.reshape(mesh.shape["row"], 4, 4), ("row", "col_0", "col_1"))
    return jax.shard_map(
        on_device,
        mesh=finer,
        in_specs=(P(COL, "row"), P("row", COL), P(COL, "row", None), P(COL)),
        out_specs=(P("row", COL), P("row", COL), P("row", COL)),
        check_vma=False,
    )
```

profile of v0, /device:TPU:1, one launch (start us, length us, event | category | flops | bytes accessed | tf_op | source)
XLA Modules:
  0.0 739.4 jit_solution(2623361062181280832)
XLA Ops:
  9.7 112.1 %all-gather.10.cloned.1.call-done = bf16[8192,896]{0,1:T(8,128)(2,1)} async-done(((bf16[512,896]{0,1:T(8,128)(2,1)}), bf16[8192,896]{0,1:T(8,128)(2,1)}) %all-gather.10.cloned.1.call-update) | async-done | bytes 14680080 | tf_op jit(solution)/shard_map/all_gather | solution.py:115
  128.4 47.7 %reduce-scatter.2.cloned.1.call-done = bf16[1024,448]{0,1:T(8,128)(2,1)} async-done(((bf16[8192,448]{0,1:T(8,128)(2,1)}), bf16[1024,448]{0,1:T(8,128)(2,1)}) %reduce-scatter.2.cloned.1.call-update) | async-done | bytes 917520 | tf_op jit(solution)/shard_map/reduce_scatter | solution.py:47
  176.1 47.5 %all-gather.12.cloned.1.call-done = bf16[8192,448]{0,1:T(8,128)(2,1)} async-done(((bf16[1024,448]{0,1:T(8,128)(2,1)}), bf16[8192,448]{0,1:T(8,128)(2,1)}) %all-gather.12.cloned.1.call-update) | async-done | bytes 7340048 | tf_op jit(solution)/shard_map/all_gather | solution.py:48
  223.6 16.8 %fusion.2 = f32[896,448]{0,1:T(8,128)S(1)} fusion(f32[896,448]{0,1:T(8,128)} %param.10, bf16[8192,448]{0,1:T(8,128)(2,1)} %all-gather.12.cloned.1.call-done, bf16[8192,896]{0,1:T(8,128)(2,1)} %all-gather.10.cloned.1.call-done, s32[896]{0:T(1024)S(1)} %fusion.114, s32[448]{0:T(512)S(1)} %fusion.125), kind=kOutput, calls=%fused_computation.13 | convolution fusion | flops 6579077120 | bytes 25236736 | tf_op jit(solution)/shard_map/dot_general | solution.py:122
  240.5 13.0 %all_gather.32 = f32[896,256]{0,1:T(8,128)} all-gather(f32[896,64]{0,1:T(8,128)S(1)} %slice.257), channel_id=1, replica_groups=mesh['row'=8,'col_0'=4,'col_1'=4] {'col_1'}, dimensions={1}, use_global_device_ids=true | all-gather | bytes 1146880 | tf_op jit(solution)/shard_map/all_gather | solution.py:54
  253.5 45.9 %all-gather.14.cloned.1.call-done = f32[896,1024]{0,1:T(8,128)} async-done(((f32[896,256]{0,1:T(8,128)}), f32[896,1024]{0,1:T(8,128)}) %all-gather.14.cloned.1.call-update) | async-done | bytes 3670032 | tf_op jit(solution)/shard_map/all_gather | solution.py:54
  311.3 13.9 %all-to-all-done = f32[8,64,512]{2,1,0:T(8,128)S(1)} async-done(((f32[8,64,512]{2,1,0:T(8,128)}), f32[8,64,512]{2,1,0:T(8,128)S(1)}, u32[]{:S(2)}, u32[]{:S(2)}) %all-to-all-start) | async-done | bytes 1048608 | tf_op jit(solution)/shard_map/all_to_all | solution.py:24
  328.9 11.7 %cholesky.286 = f32[128,128]{1,0:T(8,128)S(1)} custom-call(f32[128,128]{1,0:T(8,128)S(1)} %cholesky.426), custom_call_target="Cholesky" | custom-call | tf_op jit(solution)/shard_map/jit(cholesky)/cholesky | solution.py:88
  340.8 9.8 %custom-call.31 = f32[1,128,128]{1,2,0:T(8,128)S(1)} custom-call(f32[1,128,128]{2,1,0:T(8,128)S(1)} %get-tuple-element.79), custom_call_target="InvertDiagBlocksLowerTriangular" | custom-call | tf_op jit(solution)/shard_map/jit(cholesky)/cholesky | solution.py:88
  353.1 11.7 %cholesky.305 = f32[128,128]{1,0:T(8,128)S(1)} custom-call(f32[128,128]{1,0:T(8,128)S(1)} %cholesky.430), custom_call_target="Cholesky" | custom-call | tf_op jit(solution)/shard_map/jit(cholesky)/cholesky | solution.py:88
  364.9 10.0 %custom-call.32 = f32[1,128,128]{1,2,0:T(8,128)S(1)} custom-call(f32[1,128,128]{2,1,0:T(8,128)S(1)} %get-tuple-element.76), custom_call_target="InvertDiagBlocksLowerTriangular" | custom-call | tf_op jit(solution)/shard_map/jit(cholesky)/cholesky | solution.py:88
  376.4 11.7 %cholesky.326 = f32[128,128]{1,0:T(8,128)S(1)} custom-call(f32[128,128]{1,0:T(8,128)S(1)} %cholesky.435), custom_call_target="Cholesky" | custom-call | tf_op jit(solution)/shard_map/jit(cholesky)/cholesky | solution.py:88
  400.1 11.7 %cholesky.343 = f32[128,128]{1,0:T(8,128)S(1)} custom-call(f32[128,128]{1,0:T(8,128)S(1)} %convolution_subtract_fusion.10), custom_call_target="Cholesky" | custom-call | tf_op jit(solution)/shard_map/jit(cholesky)/cholesky | solution.py:88
  417.2 11.6 %while.8 = (s32[]{:T(128)}, f32[512,512]{1,0:T(8,128)}, s32[4,2]{0,1:T(2,128)S(1)}, f32[4,128,128]{2,1,0:T(8,128)S(1)}, s32[]{:T(128)}) while((s32[]{:T(128)}, f32[512,512]{1,0:T(8,128)}, s32[4,2]{0,1:T(2,128)S(1)}, f32[4,128,128]{2,1,0:T(8,128)S(1)}, s32[]{:T(128)}) %tuple.64), condition=%wide.while_cond, body=%wide.while_body.sunk | while | flops 2 | bytes 131181 | solution.py:89
  428.8 39.3 %custom-call.34 = f32[4,128,128]{1,2,0:T(8,128)S(1)} custom-call(f32[4,128,128]{2,1,0:T(8,128)S(1)} %get-tuple-element.34), custom_call_target="InvertDiagBlocksLowerTriangular" | custom-call | tf_op jit(solution)/shard_map/triangular_solve/custom-call.3 | solution.py:89
  491.4 10.4 %all-gather.20.cloned.1.call-done = f32[512,512]{1,0:T(8,128)} async-done(((f32[64,512]{1,0:T(8,128)}), f32[512,512]{1,0:T(8,128)}) %all-gather.20.cloned.1.call-update) | async-done | bytes 1048592 | tf_op jit(solution)/shard_map/all_gather | solution.py:139
  509.4 11.7 %cholesky.358 = f32[128,128]{1,0:T(8,128)S(1)} custom-call(f32[128,128]{1,0:T(8,128)S(1)} %cholesky.439), custom_call_target="Cholesky" | custom-call | tf_op jit(solution)/shard_map/jit(cholesky)/cholesky | solution.py:88
  535.3 12.1 %cholesky.377 = f32[128,128]{1,0:T(8,128)S(1)} custom-call(f32[128,128]{1,0:T(8,128)S(1)} %cholesky.443), custom_call_target="Cholesky" | custom-call | tf_op jit(solution)/shard_map/jit(cholesky)/cholesky | solution.py:88
  560.2 11.7 %cholesky.398 = f32[128,128]{1,0:T(8,128)S(1)} custom-call(f32[128,128]{1,0:T(8,128)S(1)} %cholesky.448), custom_call_target="Cholesky" | custom-call | tf_op jit(solution)/shard_map/jit(cholesky)/cholesky | solution.py:88
  584.8 11.9 %cholesky.415 = f32[128,128]{1,0:T(8,128)S(1)} custom-call(f32[128,128]{1,0:T(8,128)S(1)} %convolution_subtract_fusion.9), custom_call_target="Cholesky" | custom-call | tf_op jit(solution)/shard_map/jit(cholesky)/cholesky | solution.py:88
  605.0 12.0 %while.9 = (s32[]{:T(128)}, f32[512,512]{1,0:T(8,128)}, s32[4,2]{0,1:T(2,128)S(1)}, f32[4,128,128]{2,1,0:T(8,128)S(1)}, s32[]{:T(128)}) while((s32[]{:T(128)}, f32[512,512]{1,0:T(8,128)}, s32[4,2]{0,1:T(2,128)S(1)}, f32[4,128,128]{2,1,0:T(8,128)S(1)}, s32[]{:T(128)}) %tuple.88), condition=%wide.while_cond.clone, body=%wide.while_body.clone.sunk | while | flops 2 | bytes 131181 | solution.py:89
  617.8 40.1 %custom-call.38 = f32[4,128,128]{1,2,0:T(8,128)S(1)} custom-call(f32[4,128,128]{2,1,0:T(8,128)} %copy-done.8), custom_call_target="InvertDiagBlocksLowerTriangular" | custom-call | tf_op jit(solution)/shard_map/triangular_solve/custom-call.3 | solution.py:89
  679.4 13.1 %all-gather = f32[8,64,16]{1,2,0:T(8,128)S(1)} all-gather(f32[1,64,16]{1,2,0:T(8,128)S(1)} %dynamic-slice_bitcast_fusion), channel_id=1, replica_groups=mesh['row'=8,'col_0'=4,'col_1'=4] {'row'}, dimensions={0}, use_global_device_ids=true | all-gather | bytes 36864 | tf_op jit(solution)/shard_map/all_gather | solution.py:164
  699.5 13.2 %all-gather.1 = f32[8,64,16]{1,2,0:T(8,128)S(1)} all-gather(f32[1,64,16]{1,2,0:T(8,128)S(1)} %slice_bitcast_fusion.24), channel_id=1, replica_groups=mesh['row'=8,'col_0'=4,'col_1'=4] {'row'}, dimensions={0}, use_global_device_ids=true | all-gather | bytes 36864 | tf_op jit(solution)/shard_map/all_gather | solution.py:164
  (190 shorter events, 191.6 us)
Async XLA Ops:
  7.2 472.4 %copy-start = (bf16[4,896,256]{2,1,0:T(8,128)(2,1)S(1)}, bf16[4,896,256]{2,1,0:T(8,128)(2,1)}, u32[]{:S(2)}) copy-start(bf16[4,896,256]{2,1,0:T(8,128)(2,1)} %param.11) | copy-start | bytes 5505028
  7.2 114.6 %all-gather.10.cloned.1.call-start = ((), (), s32[]{:S(2)}) async-start(), calls=%async_computation.2 | async-start | bytes 15597568 | tf_op jit(solution)/shard_map/all_gather | solution.py:115
  9.6 166.5 %reduce-scatter.2.cloned.1.call-start = ((), (), s32[]{:S(2)}) async-start(), calls=%async_computation.3 | async-start | bytes 8257536 | tf_op jit(solution)/shard_map/reduce_scatter | solution.py:47
  128.3 95.3 %all-gather.12.cloned.1.call-start = ((), (), s32[]{:S(2)}) async-start(), calls=%async_computation.4 | async-start | bytes 8257536 | tf_op jit(solution)/shard_map/all_gather | solution.py:48
  176.1 123.3 %all-gather.14.cloned.1.call-start = ((), (), s32[]{:S(2)}) async-start(), calls=%async_computation.5 | async-start | bytes 4587520 | tf_op jit(solution)/shard_map/all_gather | solution.py:54
  240.4 62.6 %copy-start.6 = (f32[896,448]{0,1:T(8,128)}, f32[896,448]{0,1:T(8,128)S(1)}, u32[]{:S(2)}) copy-start(f32[896,448]{0,1:T(8,128)S(1)} %fusion.2) | copy-start | bytes 4816900
  305.0 5.3 copy-start.7
  305.0 20.2 %all-to-all-start = ((f32[8,64,512]{2,1,0:T(8,128)}), f32[8,64,512]{2,1,0:T(8,128)S(1)}, u32[]{:S(2)}, u32[]{:S(2)}) async-start(f32[8,64,512]{2,1,0:T(8,128)} %broadcast_in_dim.34), calls=%async_computation.1 | async-start | bytes 2097152 | tf_op jit(solution)/shard_map/all_to_all | solution.py:24
  310.3 178.6 %all-gather.18.cloned.1.call-start = ((), (), s32[]{:S(2)}) async-start(), calls=%async_computation.7 | async-start | bytes 1179648 | tf_op jit(solution)/shard_map/all_gather | solution.py:140
  311.1 190.7 %all-gather.20.cloned.1.call-start = ((), (), s32[]{:S(2)}) async-start(), calls=%async_computation.8 | async-start | bytes 1179648 | tf_op jit(solution)/shard_map/all_gather | solution.py:139
  327.9 1.0 copy-start.4
  477.2 2.4 copy-start.9
  477.3 1.2 copy-start.1
  479.5 199.2 %all-reduce.4.cloned.1.call-start = ((), (), s32[]{:S(2)}) async-start(), calls=%async_computation.10 | async-start | bytes 1835008
  483.6 237.7 %all-gather.16.cloned.1.call-start = ((), (), s32[]{:S(2)}) async-start(), calls=%async_computation.6 | async-start | bytes 8257536 | tf_op jit(solution)/shard_map/all_gather | solution.py:34
  488.6 237.5 %all-gather.22.cloned.1.call-start = ((), (), s32[]{:S(2)}) async-start(), calls=%async_computation.9 | async-start | bytes 8257536 | tf_op jit(solution)/shard_map/all_gather | solution.py:34
  508.4 1.0 copy-start.5
  583.2 74.7 %copy-start.3 = (f32[512,512]{1,0:T(8,128)S(1)}, f32[512,512]{1,0:T(8,128)}, u32[]{:S(2)}) copy-start(f32[512,512]{1,0:T(8,128)} %all-gather.20.cloned.1.call-done) | copy-start | bytes 3145732
  617.1 0.7 copy-start.8
  675.2 2.3 copy-start.10
  717.1 3.4 copy-start.2
Sparse Core Ops, SparseCore 0:
  10.7 111.0 all-gather.9
  128.4 47.5 reduce-scatter.1
  177.7 45.8 all-gather.11
  253.6 45.7 all-gather.13
  312.5 23.6 all-gather.17
  479.6 22.1 all-gather.19
  505.1 85.3 all-reduce.3
  592.2 46.6 all-gather.15
  677.5 45.4 all-gather.21
where the time goes:
time: 747 us; the launch traced here: 739 us
  waiting for transfers between devices  278 us (37%)
  other arithmetic  255 us (34%)
  matrix products  82.4 us (11%)
  local copies, waits for them, and re-layouts  58.1 us (8%)
  blocking collectives  39.3 us (5%)
  between operations  20.5 us (3%)
    another operation x29, other arithmetic, factor_rows(): lower_part = jnp.linalg.cholesky(diag_block)  160 us
    all_gather x1, waiting for transfers between devices, on_device(): all_tokens = lax.all_gather(activations, COL, axis=0, tiled=True)  112 us
    another operation x5, other arithmetic, factor_rows(): lax.linalg.triangular_solve(lower_part, panel_cols, left_side=False, lowe...  83 us
    reduce_scatter x1, waiting for transfers between devices, spread_2(): own = lax.psum_scatter(padded, axis, scatter_dimension=0, tiled=True)  47.7 us
    all_gather x1, waiting for transfers between devices, spread_2(): lax.all_gather(own, axis, axis=0, tiled=True)[:len(lines)]  47.5 us
    all_gather x1, waiting for transfers between devices, gather_axes(): whole = lax.all_gather(whole, axes[number], axis=dim, tiled=True)  45.9 us
    all_gather x2, blocking collectives, on_device(): gathered_rhs = lax.all_gather(rows_here, 'row', axis=0, tiled=True)  26.3 us
    another operation x27, local copies, waits for them, and re-layouts, factor_rows(): lax.linalg.triangular_solve(lower_part, panel_cols, left_side=False, lowe...  23.9 us
  transfers between devices with their start and end apart: 10, of which 6 were waited for; matrix products, arithmetic and copies ran while one was open for 48% of the time, Pallas kernels for 0%

commit v1 on v0

--- a/solution.py
+++ b/solution.py
@@ -11,6 +11,11 @@
 COL = ("col_0", "col_1")
 DECAY = 0.75
 DAMPING = 0.05
+
+
+def swapped_in(x, axis, dim):
+    sent = jnp.stack([x] * lax.axis_size(axis))
+    return jnp.concatenate(lax.all_to_all(sent, axis, 0, 0), axis=dim)
 
 
 def joined_along(parts, dim):
@@ -45,7 +50,7 @@
     )
     padded = filled_up(lines, lax.axis_size(axis))
     own = lax.psum_scatter(padded, axis, scatter_dimension=0, tiled=True)
-    return lax.all_gather(own, axis, axis=0, tiled=True)[: len(lines)].reshape(shard.shape)
+    return swapped_in(own, axis, 0)[: len(lines)].reshape(shard.shape)
 
 
 def gather_axes(shard, axes, dim):

time: 747 us -> 801 us (1.072)
  waiting for transfers between devices: 278 us -> 312 us
  local copies, waits for them, and re-layouts: 58.1 us -> 70.4 us
    all_to_all x0 -> x1, waiting for transfers between devices: none -> 82.5 us  [swapped_in(): return jnp.concatenate(lax.all_to_all(sent, axis, 0, 0), axis=dim)]
    all_gather x1 -> x0, waiting for transfers between devices: 47.5 us -> none  [spread_2(): lax.all_gather(own, axis, axis=0, tiled=True)[:len(lines)]]
  transfers between devices with their start and end apart: 10 -> 10, of which waited for: 6 -> 6; matrix products, arithmetic and copies ran while one was open for 48% -> 45% of each run, Pallas kernels for 0% -> 0%
where the time goes in v1:
time: 801 us; the launch traced here: 793 us
  waiting for transfers between devices  312 us (39%)
  other arithmetic  255 us (32%)
  matrix products  82.4 us (10%)
  local copies, waits for them, and re-layouts  70.4 us (9%)
  blocking collectives  39.3 us (5%)
  between operations  20.8 us (3%)
  starting transfers between devices  11.8 us (1%)
    another operation x29, other arithmetic, factor_rows(): lower_part = jnp.linalg.cholesky(diag_block)  160 us
    all_gather x1, waiting for transfers between devices, on_device(): all_tokens = lax.all_gather(activations, COL, axis=0, tiled=True)  112 us
    another operation x5, other arithmetic, factor_rows(): lax.linalg.triangular_solve(lower_part, panel_cols, left_side=False, lowe...  83 us
    all_to_all x1, waiting for transfers between devices, swapped_in(): return jnp.concatenate(lax.all_to_all(sent, axis, 0, 0), axis=dim)  82.5 us
    reduce_scatter x1, waiting for transfers between devices, spread_2(): own = lax.psum_scatter(padded, axis, scatter_dimension=0, tiled=True)  47.7 us
    all_gather x1, waiting for transfers between devices, gather_axes(): whole = lax.all_gather(whole, axes[number], axis=dim, tiled=True)  45.5 us
    all_gather x2, blocking collectives, on_device(): gathered_rhs = lax.all_gather(rows_here, 'row', axis=0, tiled=True)  26.1 us
    another operation x27, local copies, waits for them, and re-layouts, factor_rows(): lax.linalg.triangular_solve(lower_part, panel_cols, left_side=False, lowe...  23.7 us
  transfers between devices with their start and end apart: 10, of which 6 were waited for; matrix products, arithmetic and copies ran while one was open for 45% of the time, Pallas kernels for 0%

profile of v1, /device:TPU:1, one launch (start us, length us, event | category | flops | bytes accessed | tf_op | source)
XLA Modules:
  0.0 792.5 jit_solution(16206990921896877767)
XLA Ops:
  9.7 112.1 %all-gather.9.cloned.1.call-done = bf16[8192,896]{0,1:T(8,128)(2,1)} async-done(((bf16[512,896]{0,1:T(8,128)(2,1)}), bf16[8192,896]{0,1:T(8,128)(2,1)}) %all-gather.9.cloned.1.call-update) | async-done | bytes 14680080 | tf_op jit(solution)/shard_map/all_gather | solution.py:120
  128.3 47.7 %reduce-scatter.2.cloned.1.call-done = bf16[1024,448]{0,1:T(8,128)(2,1)} async-done(((bf16[8192,448]{0,1:T(8,128)(2,1)}), bf16[1024,448]{0,1:T(8,128)(2,1)}) %reduce-scatter.2.cloned.1.call-update) | async-done | bytes 917520 | tf_op jit(solution)/shard_map/reduce_scatter | solution.py:52
  187.1 82.5 %all-to-all-done = bf16[8,1024,448]{1,2,0:T(8,128)(2,1)} async-done(((bf16[8,1024,448]{1,2,0:T(8,128)(2,1)}), bf16[8,1024,448]{1,2,0:T(8,128)(2,1)}, u32[]{:S(2)}, u32[]{:S(2)}) %all-to-all-start) | async-done | bytes 7340064 | tf_op jit(solution)/shard_map/all_to_all | solution.py:18
  276.9 16.8 %fusion.2 = f32[896,448]{0,1:T(8,128)S(1)} fusion(f32[896,448]{0,1:T(8,128)} %param.10, bf16[8192,448]{0,1:T(8,128)(2,1)} %bitcast.187, bf16[8192,896]{0,1:T(8,128)(2,1)} %all-gather.9.cloned.1.call-done, s32[896]{0:T(1024)S(1)} %fusion.114, s32[448]{0:T(512)S(1)} %fusion.125), kind=kOutput, calls=%fused_computation.13 | convolution fusion | flops 6579077120 | bytes 25236736 | tf_op jit(solution)/shard_map/dot_general | solution.py:127
  293.8 13.1 %all_gather.28 = f32[896,256]{0,1:T(8,128)} all-gather(f32[896,64]{0,1:T(8,128)S(1)} %slice.257), channel_id=1, replica_groups=mesh['row'=8,'col_0'=4,'col_1'=4] {'col_1'}, dimensions={1}, use_global_device_ids=true | all-gather | bytes 1146880 | tf_op jit(solution)/shard_map/all_gather | solution.py:59
  307.0 45.5 %all-gather.11.cloned.1.call-done = f32[896,1024]{0,1:T(8,128)} async-done(((f32[896,256]{0,1:T(8,128)}), f32[896,1024]{0,1:T(8,128)}) %all-gather.11.cloned.1.call-update) | async-done | bytes 3670032 | tf_op jit(solution)/shard_map/all_gather | solution.py:59
  364.4 13.9 %all-to-all-done.1 = f32[8,64,512]{2,1,0:T(8,128)S(1)} async-done(((f32[8,64,512]{2,1,0:T(8,128)}), f32[8,64,512]{2,1,0:T(8,128)S(1)}, u32[]{:S(2)}, u32[]{:S(2)}) %all-to-all-start.1) | async-done | bytes 1048608 | tf_op jit(solution)/shard_map/all_to_all | solution.py:29
  382.0 11.7 %cholesky.286 = f32[128,128]{1,0:T(8,128)S(1)} custom-call(f32[128,128]{1,0:T(8,128)S(1)} %cholesky.426), custom_call_target="Cholesky" | custom-call | tf_op jit(solution)/shard_map/jit(cholesky)/cholesky | solution.py:93
  406.2 11.7 %cholesky.305 = f32[128,128]{1,0:T(8,128)S(1)} custom-call(f32[128,128]{1,0:T(8,128)S(1)} %cholesky.430), custom_call_target="Cholesky" | custom-call | tf_op jit(solution)/shard_map/jit(cholesky)/cholesky | solution.py:93
  417.9 10.0 %custom-call.32 = f32[1,128,128]{1,2,0:T(8,128)S(1)} custom-call(f32[1,128,128]{2,1,0:T(8,128)S(1)} %get-tuple-element.76), custom_call_target="InvertDiagBlocksLowerTriangular" | custom-call | tf_op jit(solution)/shard_map/jit(cholesky)/cholesky | solution.py:93
  429.5 11.7 %cholesky.326 = f32[128,128]{1,0:T(8,128)S(1)} custom-call(f32[128,128]{1,0:T(8,128)S(1)} %cholesky.435), custom_call_target="Cholesky" | custom-call | tf_op jit(solution)/shard_map/jit(cholesky)/cholesky | solution.py:93
  453.2 11.7 %cholesky.343 = f32[128,128]{1,0:T(8,128)S(1)} custom-call(f32[128,128]{1,0:T(8,128)S(1)} %convolution_subtract_fusion.10), custom_call_target="Cholesky" | custom-call | tf_op jit(solution)/shard_map/jit(cholesky)/cholesky | solution.py:93
  470.4 11.8 %while.8 = (s32[]{:T(128)}, f32[512,512]{1,0:T(8,128)}, s32[4,2]{0,1:T(2,128)S(1)}, f32[4,128,128]{2,1,0:T(8,128)S(1)}, s32[]{:T(128)}) while((s32[]{:T(128)}, f32[512,512]{1,0:T(8,128)}, s32[4,2]{0,1:T(2,128)S(1)}, f32[4,128,128]{2,1,0:T(8,128)S(1)}, s32[]{:T(128)}) %tuple.64), condition=%wide.while_cond, body=%wide.while_body.sunk | while | flops 2 | bytes 131181 | solution.py:94
  482.2 39.3 %custom-call.34 = f32[4,128,128]{1,2,0:T(8,128)S(1)} custom-call(f32[4,128,128]{2,1,0:T(8,128)S(1)} %get-tuple-element.34), custom_call_target="InvertDiagBlocksLowerTriangular" | custom-call | tf_op jit(solution)/shard_map/triangular_solve/custom-call.3 | solution.py:94
  544.9 10.4 %all-gather.17.cloned.1.call-done = f32[512,512]{1,0:T(8,128)} async-done(((f32[64,512]{1,0:T(8,128)}), f32[512,512]{1,0:T(8,128)}) %all-gather.17.cloned.1.call-update) | async-done | bytes 1048592 | tf_op jit(solution)/shard_map/all_gather | solution.py:144
  562.9 11.7 %cholesky.358 = f32[128,128]{1,0:T(8,128)S(1)} custom-call(f32[128,128]{1,0:T(8,128)S(1)} %cholesky.439), custom_call_target="Cholesky" | custom-call | tf_op jit(solution)/shard_map/jit(cholesky)/cholesky | solution.py:93
  588.8 12.1 %cholesky.377 = f32[128,128]{1,0:T(8,128)S(1)} custom-call(f32[128,128]{1,0:T(8,128)S(1)} %cholesky.443), custom_call_target="Cholesky" | custom-call | tf_op jit(solution)/shard_map/jit(cholesky)/cholesky | solution.py:93
  601.5 9.8 %custom-call.36 = f32[1,128,128]{1,2,0:T(8,128)S(1)} custom-call(f32[1,128,128]{2,1,0:T(8,128)S(1)} %get-tuple-element.66), custom_call_target="InvertDiagBlocksLowerTriangular" | custom-call | tf_op jit(solution)/shard_map/jit(cholesky)/cholesky | solution.py:93
  613.7 11.7 %cholesky.398 = f32[128,128]{1,0:T(8,128)S(1)} custom-call(f32[128,128]{1,0:T(8,128)S(1)} %cholesky.448), custom_call_target="Cholesky" | custom-call | tf_op jit(solution)/shard_map/jit(cholesky)/cholesky | solution.py:93
  638.2 11.9 %cholesky.415 = f32[128,128]{1,0:T(8,128)S(1)} custom-call(f32[128,128]{1,0:T(8,128)S(1)} %convolution_subtract_fusion.9), custom_call_target="Cholesky" | custom-call | tf_op jit(solution)/shard_map/jit(cholesky)/cholesky | solution.py:93
  658.4 11.6 %while.9 = (s32[]{:T(128)}, f32[512,512]{1,0:T(8,128)}, s32[4,2]{0,1:T(2,128)S(1)}, f32[4,128,128]{2,1,0:T(8,128)S(1)}, s32[]{:T(128)}) while((s32[]{:T(128)}, f32[512,512]{1,0:T(8,128)}, s32[4,2]{0,1:T(2,128)S(1)}, f32[4,128,128]{2,1,0:T(8,128)S(1)}, s32[]{:T(128)}) %tuple.86), condition=%wide.while_cond.clone, body=%wide.while_body.clone.sunk | while | flops 2 | bytes 131181 | solution.py:94
  670.7 40.1 %custom-call.38 = f32[4,128,128]{1,2,0:T(8,128)S(1)} custom-call(f32[4,128,128]{2,1,0:T(8,128)} %copy-done.8), custom_call_target="InvertDiagBlocksLowerTriangular" | custom-call | tf_op jit(solution)/shard_map/triangular_solve/custom-call.3 | solution.py:94
  732.3 13.0 %all-gather = f32[8,64,16]{1,2,0:T(8,128)S(1)} all-gather(f32[1,64,16]{1,2,0:T(8,128)S(1)} %dynamic-slice_bitcast_fusion), channel_id=1, replica_groups=mesh['row'=8,'col_0'=4,'col_1'=4] {'row'}, dimensions={0}, use_global_device_ids=true | all-gather | bytes 36864 | tf_op jit(solution)/shard_map/all_gather | solution.py:169
  752.4 13.1 %all-gather.1 = f32[8,64,16]{1,2,0:T(8,128)S(1)} all-gather(f32[1,64,16]{1,2,0:T(8,128)S(1)} %slice_bitcast_fusion.24), channel_id=1, replica_groups=mesh['row'=8,'col_0'=4,'col_1'=4] {'row'}, dimensions={0}, use_global_device_ids=true | all-gather | bytes 36864 | tf_op jit(solution)/shard_map/all_gather | solution.py:169
  (191 shorter events, 209.9 us)
Async XLA Ops:
  7.2 525.8 %copy-start = (bf16[4,896,256]{2,1,0:T(8,128)(2,1)S(1)}, bf16[4,896,256]{2,1,0:T(8,128)(2,1)}, u32[]{:S(2)}) copy-start(bf16[4,896,256]{2,1,0:T(8,128)(2,1)} %param.11) | copy-start | bytes 5505028
  7.2 114.6 %all-gather.9.cloned.1.call-start = ((), (), s32[]{:S(2)}) async-start(), calls=%async_computation.3 | async-start | bytes 15597568 | tf_op jit(solution)/shard_map/all_gather | solution.py:120
  9.6 166.5 %reduce-scatter.2.cloned.1.call-start = ((), (), s32[]{:S(2)}) async-start(), calls=%async_computation.4 | async-start | bytes 8257536 | tf_op jit(solution)/shard_map/reduce_scatter | solution.py:52
  181.2 88.5 %all-to-all-start = ((bf16[8,1024,448]{1,2,0:T(8,128)(2,1)}), bf16[8,1024,448]{1,2,0:T(8,128)(2,1)}, u32[]{:S(2)}, u32[]{:S(2)}) async-start(bf16[8,1024,448]{1,2,0:T(8,128)(2,1)} %stack.2), calls=%async_computation.1 | async-start | bytes 14680064 | tf_op jit(solution)/shard_map/all_to_all | solution.py:18
  187.1 165.3 %all-gather.11.cloned.1.call-start = ((), (), s32[]{:S(2)}) async-start(), calls=%async_computation.5 | async-start | bytes 4587520 | tf_op jit(solution)/shard_map/all_gather | solution.py:59
  293.8 62.3 %copy-start.6 = (f32[896,448]{0,1:T(8,128)}, f32[896,448]{0,1:T(8,128)S(1)}, u32[]{:S(2)}) copy-start(f32[896,448]{0,1:T(8,128)S(1)} %fusion.2) | copy-start | bytes 4816900
  358.1 5.3 copy-start.7
  358.1 20.2 %all-to-all-start.1 = ((f32[8,64,512]{2,1,0:T(8,128)}), f32[8,64,512]{2,1,0:T(8,128)S(1)}, u32[]{:S(2)}, u32[]{:S(2)}) async-start(f32[8,64,512]{2,1,0:T(8,128)} %broadcast_in_dim.34), calls=%async_computation.2 | async-start | bytes 2097152 | tf_op jit(solution)/shard_map/all_to_all | solution.py:29
  363.3 179.0 %all-gather.15.cloned.1.call-start = ((), (), s32[]{:S(2)}) async-start(), calls=%async_computation.7 | async-start | bytes 1179648 | tf_op jit(solution)/shard_map/all_gather | solution.py:145
  364.1 191.1 %all-gather.17.cloned.1.call-start = ((), (), s32[]{:S(2)}) async-start(), calls=%async_computation.8 | async-start | bytes 1179648 | tf_op jit(solution)/shard_map/all_gather | solution.py:144
  381.0 1.0 copy-start.4
  530.6 2.4 copy-start.9
  530.7 1.2 copy-start.1
  532.9 198.7 %all-reduce.4.cloned.1.call-start = ((), (), s32[]{:S(2)}) async-start(), calls=%async_computation.10 | async-start | bytes 1835008
  537.0 237.0 %all-gather.13.cloned.1.call-start = ((), (), s32[]{:S(2)}) async-start(), calls=%async_computation.6 | async-start | bytes 8257536 | tf_op jit(solution)/shard_map/all_gather | solution.py:39
  542.0 236.8 %all-gather.19.cloned.1.call-start = ((), (), s32[]{:S(2)}) async-start(), calls=%async_computation.9 | async-start | bytes 8257536 | tf_op jit(solution)/shard_map/all_gather | solution.py:39
  561.9 1.0 copy-start.5
  636.7 74.1 %copy-start.3 = (f32[512,512]{1,0:T(8,128)S(1)}, f32[512,512]{1,0:T(8,128)}, u32[]{:S(2)}) copy-start(f32[512,512]{1,0:T(8,128)} %all-gather.17.cloned.1.call-done) | copy-start | bytes 3145732
  670.0 0.7 copy-start.8
  728.1 2.2 copy-start.10
  769.8 3.4 copy-start.2
Sparse Core Ops, SparseCore 0:
  10.7 111.0 all-gather.8
  128.5 47.5 reduce-scatter.1
  307.1 45.3 all-gather.10
  365.5 23.6 all-gather.14
  533.0 22.1 all-gather.16
  558.4 85.0 all-reduce.3
  645.2 46.5 all-gather.12
  730.4 45.5 all-gather.18
